TPU v7x, 32 devices: a whole 2x2x4 slice. The times are simulated.
32 devices in a mesh: groups: 2 (over x), sph: 16 (over z, y, core).
Axes of the slice: x: 2, y: 2, z: 4, core: 2. Of those that a mesh axis runs over, the one named last changes fastest.
Arguments:
- positions: float32 [512, 3], P('sph'), may hold values from -8 to 8
- wave_vectors: float32 [256, 3], replicated, may hold values from -5 to 5
- pattern: float32 [2, 448, 256], replicated, may hold values from -6 to 6
- dir_index: int32 [64], P('groups'), parts along dimension 0, may hold values from 0 to 255
- mie: float32 [2, 448, 512], P(None, None, 'sph'), may hold values from -0.9 to 0.9
- trans_table: bfloat16 [8, 2, 448, 448], replicated, may hold values from -0.1875 to 0.1875
- pair_route: int32 [1024, 1], P('sph'), may hold values from 0 to 15; in each aligned block of 64 rows (0 to 63, 64 to 127, ...) at most 8 rows name the same one
- pair_source: int32 [1024], P('sph'), may hold values from 0 to 15
- pair_target: int32 [1024], P('sph'), may hold values from 0 to 15
- pair_class: int32 [1024], P('sph'), may hold values from 0 to 7
Outputs:
- scattered: bfloat16 [896, 32768], P(None, ('groups', 'sph')), parts along dimension 1
- extinction: float32 [64], P('groups'), parts along dimension 0
There are 2 independent parts, one for each index of `groups`. A program takes and returns all parts, laid end to end along the dimension named above; an argument that names none is the same for every part. Nothing has to cross between parts.
Inputs may be any that keep to these rules, and one draw needn't show every extreme that they name: `pair_route`: among the rows of one device no device is named by more than 8 pairs, and in every draw some device is named by exactly 8 of them.
All inputs are finite; a program needn't handle non-finite values.
Results may differ from a plain program's by a relative error of at most 0.0051.
Values may be sent and summed in bfloat16 or wider, within the bound.
No kernel may reach another device: no remote copies, remote signals or barrier semaphores. Data moves between devices by JAX's collectives and lax.ppermute only.
A program may use at most 192 MiB of HBM per device.

v0:
```python
import jax
import jax.numpy as jnp
from jax import lax
from jax.sharding import PartitionSpec as P

BLOCK = 2
HIGHEST_PRECISION = lax.Precision.HIGHEST


def incident_field(positions, wave_vectors, pattern, dir_index):
    table_rows = wave_vectors.shape[0]
    select = (jnp.arange(table_rows, dtype=jnp.int32)[:, None] == dir_index[None, :]).astype(
        jnp.float32
    )
    directions = jnp.dot(select.T, wave_vectors, precision=HIGHEST_PRECISION)
    phases = (
        positions[:, 0:1] * directions[None, :, 0]
        + positions[:, 1:2] * directions[None, :, 1]
        + positions[:, 2:3] * directions[None, :, 2]
    )
    cosine = jnp.cos(phases)
    sine_part = jnp.sin(phases)
    chosen = jnp.einsum("cmt,td->cmd", pattern, select, precision=HIGHEST_PRECISION)
    inc_real = cosine[None] * chosen[0][:, None, :] - sine_part[None] * chosen[1][:, None, :]
    inc_imag = cosine[None] * chosen[1][:, None, :] + sine_part[None] * chosen[0][:, None, :]
    return (inc_real, inc_imag)


def translate(trans_table, classes, block_values):
    item_count = classes.shape[0]
    mode_count = trans_table.shape[2]
    grouped_classes = classes.reshape(item_count // 8, 8)
    grouped_values = block_values.reshape((item_count // 8, 8) + block_values.shape[1:])

    def one_group(group_items):
        picked, values = group_items
        tables = trans_table[picked]
        data_real = values[:, :mode_count]
        data_imag = values[:, mode_count:]
        part_real = jnp.einsum(
            "kij,kjc->kic", tables[:, 0], data_real, preferred_element_type=jnp.float32
        ) - jnp.einsum("kij,kjc->kic", tables[:, 1], data_imag, preferred_element_type=jnp.float32)
        part_imag = jnp.einsum(
            "kij,kjc->kic", tables[:, 1], data_real, preferred_element_type=jnp.float32
        ) + jnp.einsum("kij,kjc->kic", tables[:, 0], data_imag, preferred_element_type=jnp.float32)
        return jnp.concatenate([part_real, part_imag], 1).astype(jnp.bfloat16)

    return lax.map(one_group, (grouped_classes, grouped_values)).reshape(block_values.shape)


def shards(
    positions,
    wave_vectors,
    pattern,
    dir_index,
    mie,
    trans_table,
    pair_route,
    pair_source,
    pair_target,
    pair_class,
):
    mode_count = pattern.shape[1]
    spheres = positions.shape[0]
    directions = dir_index.shape[0]
    columns = BLOCK * directions
    block_count = spheres // BLOCK
    devices = lax.axis_size("sph")
    pair_count = pair_source.shape[0]
    capacity = max(2, 2 * pair_count // devices)
    slot_count = devices * capacity
    inc_real, inc_imag = incident_field(positions, wave_vectors, pattern, dir_index)
    mie_real = mie[0][:, :, None]
    mie_imag = mie[1][:, :, None]
    scat_real = mie_real * inc_real - mie_imag * inc_imag
    scat_imag = mie_real * inc_imag + mie_imag * inc_real
    coeffs = jnp.concatenate([scat_real, scat_imag], 0).astype(jnp.bfloat16)
    block_data = coeffs.reshape(2 * mode_count, block_count, columns).transpose(1, 0, 2)
    dest_device = pair_route[:, 0]
    by_device = (dest_device[:, None] == jnp.arange(devices, dtype=jnp.int32)[None, :]).astype(
        jnp.int32
    )
    before = jnp.cumsum(by_device, axis=0) - by_device
    rank_in = jnp.sum(before * by_device, axis=1)
    slot_of = dest_device * capacity + rank_in
    slot_match = (jnp.arange(slot_count, dtype=jnp.int32)[:, None] == slot_of[None, :]).astype(
        jnp.int32
    )
    filled = jnp.sum(slot_match, axis=1)
    slot_pair = jnp.sum(slot_match * jnp.arange(pair_count, dtype=jnp.int32)[None, :], axis=1)
    slot_target = jnp.where(filled > 0, pair_target[slot_pair], -1)
    keep_slot = filled.astype(jnp.bfloat16)[:, None, None]
    computed = translate(trans_table, pair_class, block_data[pair_source])
    outgoing = computed[slot_pair] * keep_slot
    outgoing = outgoing.reshape(devices, capacity, 2 * mode_count, columns)
    arrived = lax.all_to_all(outgoing, "sph", split_axis=0, concat_axis=0, tiled=True)
    targets = lax.all_to_all(
        slot_target.reshape(devices, capacity), "sph", split_axis=0, concat_axis=0, tiled=True
    ).reshape(slot_count)
    partial_value = arrived.reshape(slot_count, 2 * mode_count, columns)
    gather_matrix = (jnp.arange(block_count, dtype=jnp.int32)[:, None] == targets[None, :]).astype(
        jnp.bfloat16
    )
    summed = jnp.dot(
        gather_matrix,
        partial_value.reshape(slot_count, 2 * mode_count * columns),
        preferred_element_type=jnp.float32,
    )
    summed = (
        summed.reshape(block_count, 2 * mode_count, columns)
        .transpose(1, 0, 2)
        .reshape(2 * mode_count, spheres, directions)
    )
    total_real = inc_real + summed[:mode_count]
    total_imag = inc_imag + summed[mode_count:]
    out_real = mie_real * total_real - mie_imag * total_imag
    out_imag = mie_real * total_imag + mie_imag * total_real
    scattered = (
        jnp.concatenate([out_real, out_imag], 0)
        .reshape(2 * mode_count, spheres * directions)
        .astype(jnp.bfloat16)
    )
    local_ext = jnp.sum(inc_real * out_real + inc_imag * out_imag, axis=(0, 1))
    extinction = lax.psum(local_ext, "sph")
    return (scattered, extinction)


def solution(mesh):
    placed = (
        P("sph", None),
        P(),
        P(),
        P("groups"),
        P(None, None, "sph"),
        P(),
        P("sph", None),
        P("sph"),
        P("sph"),
        P("sph"),
    )
    return jax.shard_map(
        shards,
        mesh=mesh,
        in_specs=placed,
        out_specs=(P(None, ("groups", "sph")), P("groups")),
        check_vma=False,
    )
```

profile of v0, /device:TPU:0, one launch (start us, length us, event | category | flops | bytes accessed | tf_op | source)
XLA Modules:
  0.0 671.2 jit_solution(2450275542576880069)
XLA Ops:
  5.5 7.4 %all-to-all-start = ((s32[16,1,8]{2,1,0:T(1,128)}), s32[16,1,8]{2,1,0:T(1,128)S(1)}, u32[]{:S(2)}, u32[]{:S(2)}) async-start(s32[16,1,8]{2,1,0:T(1,128)} %bitcast.24), calls=%async_computation | async-start | bytes 16384 | tf_op jit(solution)/shard_map/all_to_all | solution.py:97
  21.9 4.3 gather_fusion.2
  26.3 134.5 %while.10 = (s32[]{:T(128)}, bf16[8,8,896,64]{2,3,1,0:T(8,128)(2,1)}, s32[8,8]{1,0:T(8,128)S(1)}, bf16[8,2,448,448]{3,2,1,0:T(8,128)(2,1)}, bf16[8,8,896,64]{2,3,1,0:T(8,128)(2,1)}, /*index=5*/s32[]{:T(128)}) while((s32[]{:T(128)}, bf16[8,8,896,64]{2,3,1,0:T(8,128)(2,1)}, s32[8,8]{1,0:T(8,128)S(1)}, bf16[8,2,448,448]{3,2,1,0:T(8,128)(2,1)}, ...), condition=%wide.region_5.6_spmd, body=%wide.region_4.5_spmd.sunk | while | flops 824837120 | bytes 63836904 | solution.py:48
  26.3 7.0 %gather_fusion = bf16[8,2,448,448]{3,2,1,0:T(8,128)(2,1)} fusion(bf16[8,2,448,448]{3,2,1,0:T(8,128)(2,1)} %get-tuple-element.133, s32[1024]{0:T(1024)S(1)} %pad_clamp_fusion.4), kind=kCustom, calls=%fused_computation.clone.1 | custom fusion | bytes 12845088 | tf_op jit(solution)/shard_map/while/body/eval_jaxpr/gather | solution.py:37
  43.1 7.0 %gather_fusion = bf16[8,2,448,448]{3,2,1,0:T(8,128)(2,1)} fusion(bf16[8,2,448,448]{3,2,1,0:T(8,128)(2,1)} %get-tuple-element.133, s32[1024]{0:T(1024)S(1)} %pad_clamp_fusion.4), kind=kCustom, calls=%fused_computation.clone.1 | custom fusion | bytes 12845088 | tf_op jit(solution)/shard_map/while/body/eval_jaxpr/gather | solution.py:37
  51.5 3.5 fusion.68
  59.9 7.0 %gather_fusion = bf16[8,2,448,448]{3,2,1,0:T(8,128)(2,1)} fusion(bf16[8,2,448,448]{3,2,1,0:T(8,128)(2,1)} %get-tuple-element.133, s32[1024]{0:T(1024)S(1)} %pad_clamp_fusion.4), kind=kCustom, calls=%fused_computation.clone.1 | custom fusion | bytes 12845088 | tf_op jit(solution)/shard_map/while/body/eval_jaxpr/gather | solution.py:37
  68.3 3.5 fusion.68
  76.7 7.0 %gather_fusion = bf16[8,2,448,448]{3,2,1,0:T(8,128)(2,1)} fusion(bf16[8,2,448,448]{3,2,1,0:T(8,128)(2,1)} %get-tuple-element.133, s32[1024]{0:T(1024)S(1)} %pad_clamp_fusion.4), kind=kCustom, calls=%fused_computation.clone.1 | custom fusion | bytes 12845088 | tf_op jit(solution)/shard_map/while/body/eval_jaxpr/gather | solution.py:37
  93.5 7.0 %gather_fusion = bf16[8,2,448,448]{3,2,1,0:T(8,128)(2,1)} fusion(bf16[8,2,448,448]{3,2,1,0:T(8,128)(2,1)} %get-tuple-element.133, s32[1024]{0:T(1024)S(1)} %pad_clamp_fusion.4), kind=kCustom, calls=%fused_computation.clone.1 | custom fusion | bytes 12845088 | tf_op jit(solution)/shard_map/while/body/eval_jaxpr/gather | solution.py:37
  101.9 3.5 fusion.68
  110.3 7.0 %gather_fusion = bf16[8,2,448,448]{3,2,1,0:T(8,128)(2,1)} fusion(bf16[8,2,448,448]{3,2,1,0:T(8,128)(2,1)} %get-tuple-element.133, s32[1024]{0:T(1024)S(1)} %pad_clamp_fusion.4), kind=kCustom, calls=%fused_computation.clone.1 | custom fusion | bytes 12845088 | tf_op jit(solution)/shard_map/while/body/eval_jaxpr/gather | solution.py:37
  127.1 7.0 %gather_fusion = bf16[8,2,448,448]{3,2,1,0:T(8,128)(2,1)} fusion(bf16[8,2,448,448]{3,2,1,0:T(8,128)(2,1)} %get-tuple-element.133, s32[1024]{0:T(1024)S(1)} %pad_clamp_fusion.4), kind=kCustom, calls=%fused_computation.clone.1 | custom fusion | bytes 12845088 | tf_op jit(solution)/shard_map/while/body/eval_jaxpr/gather | solution.py:37
  144.0 7.0 %gather_fusion = bf16[8,2,448,448]{3,2,1,0:T(8,128)(2,1)} fusion(bf16[8,2,448,448]{3,2,1,0:T(8,128)(2,1)} %get-tuple-element.133, s32[1024]{0:T(1024)S(1)} %pad_clamp_fusion.4), kind=kCustom, calls=%fused_computation.clone.1 | custom fusion | bytes 12845088 | tf_op jit(solution)/shard_map/while/body/eval_jaxpr/gather | solution.py:37
  160.7 12.3 %gather_fusion.3 = bf16[128,896,64]{1,2,0:T(8,128)(2,1)} fusion(bf16[64,896,64]{1,2,0:T(8,128)(2,1)} %bitcast.33, s32[1024]{0:T(1024)S(1)} %pad_clamp_fusion.2), kind=kCustom, calls=%fused_computation.3 | custom fusion | bytes 29360640 | tf_op jit(solution)/shard_map/gather | solution.py:94
  173.1 13.5 %broadcast_multiply_fusion = bf16[16,8,896,64]{2,3,1,0:T(8,128)(2,1)} fusion(bf16[16,8,896,64]{2,3,1,0:T(8,128)(2,1)} %bitcast.236, bf16[16,8]{1,0:T(8,128)(2,1)S(1)} %convert_element_type.32), kind=kLoop, calls=%fused_computation.29 | loop fusion | flops 7340032 | bytes 29360384 | tf_op jit(solution)/shard_map/mul | solution.py:94
  186.6 6.0 all-to-all-start.1
  194.7 258.1 %all-to-all-done.1 = bf16[16,8,896,64]{2,3,1,0:T(8,128)(2,1)} async-done(((bf16[16,8,896,64]{2,3,1,0:T(8,128)(2,1)}), bf16[16,8,896,64]{2,3,1,0:T(8,128)(2,1)}, u32[]{:S(2)}, u32[]{:S(2)}) %all-to-all-start.1) | async-done | bytes 14680096 | tf_op jit(solution)/shard_map/all_to_all | solution.py:96
  452.8 26.5 %copy.80 = bf16[16,8,896,64]{3,2,1,0:T(8,128)(2,1)} copy(bf16[16,8,896,64]{2,3,1,0:T(8,128)(2,1)} %all-to-all-done.1) | data formatting | bytes 29360128 | tf_op jit(solution)/shard_map/all_to_all | solution.py:96
  479.3 28.1 %reshape_reshape.3 = bf16[128,57344]{1,0:T(8,128)(2,1)} reshape(bf16[16,8,896,64]{3,2,1,0:T(8,128)(2,1)} %copy.80) | data formatting | bytes 29360128 | tf_op jit(solution)/shard_map/reshape;reshape | solution.py:106
  507.4 20.2 %copy.81 = bf16[57344,128]{1,0:T(8,128)(2,1)} copy(bf16[57344,128]{0,1:T(8,128)(2,1)} %bitcast.238) | data formatting | bytes 29360128 | tf_op jit(solution)/shard_map/dot_general | solution.py:104
  527.6 35.5 %fusion.34 = f32[896,16,64]{0,1,2:T(8,128)} fusion(bf16[896,64,128]{2,1,0:T(8,128)(2,1)} %bitcast.237, s32[128]{0:T(128)S(1)} %eq.64), kind=kOutput, calls=%fused_computation.61 | convolution fusion | flops 234883072 | bytes 18350592 | tf_op jit(solution)/shard_map/dot_general | solution.py:104
  563.1 9.9 %add_reduce_fusion = (f32[16,64]{0,1:T(8,128)S(1)}, f32[448,16,64]{0,1,2:T(8,128)S(1)}, f32[448,16,64]{0,1,2:T(8,128)S(1)}) fusion(f32[448,16,64]{0,2,1:T(8,128)S(1)} %bitcast.241, f32[448,16,64]{0,2,1:T(8,128)} %bitcast.247, f32[448,16,64]{0,2,1:T(8,128)S(1)} %bitcast.243, f32[448,16,64]{0,2,1:T(8,128)S(1)} %bitcast.245, f32[16,64]{0,1:T(8,128)S(1)} %copy.87, ...), kind=kLoop, calls=%fused_computation.60 | loop fusion | flops 8256512 | bytes 14692352 | tf_op jit(solution)/shard_map/reduce_sum | solution.py:123
  580.4 90.4 %psum.7 = f32[32]{0:T(128)} all-reduce(f32[32]{0:T(128)S(1)} %reduce_sum.51), channel_id=1, replica_groups=mesh['groups'=2,'sph'=16] {'sph'}, use_global_device_ids=true, to_apply=%region_8.9 | all-reduce | flops 32 | bytes 256 | tf_op jit(solution)/shard_map/psum | solution.py:124
  (192 shorter events, 90.8 us)
Async XLA Ops:
  0.6 15.6 %copy-start = (f32[2,448,256]{2,1,0:T(8,128)S(1)}, f32[2,448,256]{2,1,0:T(8,128)}, u32[]{:S(2)}) copy-start(f32[2,448,256]{2,1,0:T(8,128)} %param.14) | copy-start | bytes 2752516
  0.6 16.9 %copy-start.20 = (s32[64]{0:T(128)S(1)}, s32[64]{0:T(128)}, u32[]{:S(2)}) copy-start(s32[64]{0:T(128)} %param.19) | copy-start | bytes 772
  0.7 16.9 %copy-start.19 = (s32[64]{0:T(128)S(1)}, s32[64]{0:T(128)}, u32[]{:S(2)}) copy-start(s32[64]{0:T(128)} %param.21) | copy-start | bytes 772
  0.7 17.0 %copy-start.18 = (f32[2,448,32]{1,2,0:T(8,128)S(1)}, f32[2,448,32]{1,2,0:T(8,128)}, u32[]{:S(2)}) copy-start(f32[2,448,32]{1,2,0:T(8,128)} %param.16) | copy-start | bytes 344068
  5.5 181.1 %all-to-all-start = ((s32[16,1,8]{2,1,0:T(1,128)}), s32[16,1,8]{2,1,0:T(1,128)S(1)}, u32[]{:S(2)}, u32[]{:S(2)}) async-start(s32[16,1,8]{2,1,0:T(1,128)} %bitcast.24), calls=%async_computation | async-start | bytes 16384 | tf_op jit(solution)/shard_map/all_to_all | solution.py:97
  18.0 1.3 copy-start.3
  18.3 1.7 copy-start.5
  18.6 2.5 copy-start.7
  18.9 2.5 copy-start.9
  33.3 4.9 copy-start.2
  50.1 4.9 copy-start.2
  66.9 4.9 copy-start.2
  83.7 4.9 copy-start.2
  100.5 4.9 copy-start.2
  117.3 4.9 copy-start.2
  134.1 4.9 copy-start.2
  151.0 4.9 copy-start.2
  186.6 266.2 %all-to-all-start.1 = ((bf16[16,8,896,64]{2,3,1,0:T(8,128)(2,1)}), bf16[16,8,896,64]{2,3,1,0:T(8,128)(2,1)}, u32[]{:S(2)}, u32[]{:S(2)}) async-start(bf16[16,8,896,64]{2,3,1,0:T(8,128)(2,1)} %broadcast_multiply_fusion), calls=%async_computation.1 | async-start | bytes 29360128 | tf_op jit(solution)/shard_map/all_to_all | solution.py:96
  527.6 35.5 %copy-start.4 = (f32[448,32,32]{0,2,1:T(8,128)S(1)}, f32[448,32,32]{0,2,1:T(8,128)}, u32[]{:S(2)}) copy-start(f32[448,32,32]{0,2,1:T(8,128)} %copy-done.3) | copy-start | bytes 5505028
  527.6 35.5 %copy-start.6 = (f32[448,32,32]{0,2,1:T(8,128)S(1)}, f32[448,32,32]{0,2,1:T(8,128)}, u32[]{:S(2)}) copy-start(f32[448,32,32]{0,2,1:T(8,128)} %copy-done.5) | copy-start | bytes 5505028
  527.6 35.5 %copy-start.8 = (f32[448,32,32]{0,2,1:T(8,128)S(1)}, f32[448,32,32]{0,2,1:T(8,128)}, u32[]{:S(2)}) copy-start(f32[448,32,32]{0,2,1:T(8,128)} %copy-done.7) | copy-start | bytes 5505028
  574.3 1.3 copy-start.11
  574.3 1.3 copy-start.13
  577.2 93.6 %copy-start.1 = (f32[2,448,256]{2,1,0:T(8,128)S(1)}, f32[2,448,256]{2,1,0:T(8,128)}, u32[]{:S(2)}) copy-start(f32[2,448,256]{2,1,0:T(8,128)} %param.14) | copy-start | bytes 2752516
  (6 other events, 5.3 us)
where the time goes:
time: 683 us; the launch traced here: 671 us
  waiting for transfers between devices  258 us (38%)
  local copies, waits for them, and re-layouts  172 us (25%)
  matrix products  94.1 us (14%)
  blocking collectives  90.4 us (13%)
  other arithmetic  41 us (6%)
  starting transfers between devices  13.5 us (2%)
    all_to_all x1, waiting for transfers between devices, shards(): lax.all_to_all(outgoing, 'sph', split_axis=0, concat_axis=0, tiled=True)  258 us
    psum x1, blocking collectives, shards(): extinction = lax.psum(local_ext, 'sph')  90.4 us
    gather x8, local copies, waits for them, and re-layouts, one_group(): tables = trans_table[picked]  56.2 us
    dot_general x1, matrix products, shards(): jnp.dot(gather_matrix, partial_value.reshape(slot_count, 2 * mode_count *...  35.5 us
    another operation x1, local copies, waits for them, and re-layouts, shards(): partial_value.reshape(slot_count, 2 * mode_count * columns)  28.1 us
    dot_general x8, matrix products, one_group(): jnp.einsum('kij,kjc->kic', tables[:, 0], data_real, preferred_element_typ...  27.6 us
    all_to_all x1, local copies, waits for them, and re-layouts, shards(): lax.all_to_all(outgoing, 'sph', split_axis=0, concat_axis=0, tiled=True)  26.5 us
    dot_general x1, local copies, waits for them, and re-layouts, shards(): jnp.dot(gather_matrix, partial_value.reshape(slot_count, 2 * mode_count *...  20.2 us
  transfers between devices with their start and end apart: 2, of which 1 were waited for; matrix products, arithmetic and copies ran while one was open for 26% of the time, Pallas kernels for 0%

commit v1 on v0

--- a/solution.py
+++ b/solution.py
@@ -121,7 +121,11 @@
         .astype(jnp.bfloat16)
     )
     local_ext = jnp.sum(inc_real * out_real + inc_imag * out_imag, axis=(0, 1))
-    extinction = lax.psum(local_ext, "sph")
+    extinction = local_ext
+    for hop in (1, 2, 4, 8):
+        extinction = extinction + lax.ppermute(
+            extinction, "sph", [(dev, dev ^ hop) for dev in range(16)]
+        )
     return (scattered, extinction)
 
 

time: 683 us -> 660 us (0.966)
  blocking collectives: 90.4 us -> 0 us
  starting transfers between devices: 13.5 us -> 77.6 us
    psum x1 -> x0, blocking collectives: 90.4 us -> none  [shards(): extinction = lax.psum(local_ext, 'sph')]
    ppermute x0 -> x4, starting transfers between devices: none -> 64.1 us  [shards(): lax.ppermute(extinction, 'sph', [(dev, dev ^ hop) for dev in range(16)])]
  transfers between devices with their start and end apart: 2 -> 6, of which waited for: 1 -> 2; matrix products, arithmetic and copies ran while one was open for 26% -> 28% of each run, Pallas kernels for 0% -> 0%
where the time goes in v1:
time: 660 us; the launch traced here: 649 us
  waiting for transfers between devices  258 us (39%)
  local copies, waits for them, and re-layouts  174 us (26%)
  matrix products  94.1 us (14%)
  starting transfers between devices  77.6 us (12%)
  other arithmetic  42.9 us (6%)
    all_to_all x1, waiting for transfers between devices, shards(): lax.all_to_all(outgoing, 'sph', split_axis=0, concat_axis=0, tiled=True)  258 us
    ppermute x4, starting transfers between devices, shards(): lax.ppermute(extinction, 'sph', [(dev, dev ^ hop) for dev in range(16)])  64.1 us
    gather x8, local copies, waits for them, and re-layouts, one_group(): tables = trans_table[picked]  56.1 us
    dot_general x1, matrix products, shards(): jnp.dot(gather_matrix, partial_value.reshape(slot_count, 2 * mode_count *...  35.5 us
    another operation x1, local copies, waits for them, and re-layouts, shards(): partial_value.reshape(slot_count, 2 * mode_count * columns)  28.1 us
    dot_general x8, matrix products, one_group(): jnp.einsum('kij,kjc->kic', tables[:, 0], data_real, preferred_element_typ...  27.6 us
    all_to_all x1, local copies, waits for them, and re-layouts, shards(): lax.all_to_all(outgoing, 'sph', split_axis=0, concat_axis=0, tiled=True)  26.5 us
    dot_general x1, local copies, waits for them, and re-layouts, shards(): jnp.dot(gather_matrix, partial_value.reshape(slot_count, 2 * mode_count *...  20.1 us
  transfers between devices with their start and end apart: 6, of which 2 were waited for; matrix products, arithmetic and copies ran while one was open for 28% of the time, Pallas kernels for 0%

profile of v1, /device:TPU:0, one launch (start us, length us, event | category | flops | bytes accessed | tf_op | source)
XLA Modules:
  0.0 648.7 jit_solution(17065103738715006862)
XLA Ops:
  5.5 7.4 %all-to-all-start = ((s32[16,1,8]{2,1,0:T(1,128)}), s32[16,1,8]{2,1,0:T(1,128)S(1)}, u32[]{:S(2)}, u32[]{:S(2)}) async-start(s32[16,1,8]{2,1,0:T(1,128)} %bitcast.24), calls=%async_computation | async-start | bytes 16384 | tf_op jit(solution)/shard_map/all_to_all | solution.py:97
  21.9 4.3 gather_fusion.2
  26.2 134.4 %while.10 = (s32[]{:T(128)}, bf16[8,8,896,64]{2,3,1,0:T(8,128)(2,1)}, s32[8,8]{1,0:T(8,128)S(1)}, bf16[8,2,448,448]{3,2,1,0:T(8,128)(2,1)}, bf16[8,8,896,64]{2,3,1,0:T(8,128)(2,1)}, /*index=5*/s32[]{:T(128)}) while((s32[]{:T(128)}, bf16[8,8,896,64]{2,3,1,0:T(8,128)(2,1)}, s32[8,8]{1,0:T(8,128)S(1)}, bf16[8,2,448,448]{3,2,1,0:T(8,128)(2,1)}, ...), condition=%wide.region_5.6_spmd, body=%wide.region_4.5_spmd.sunk | while | flops 824837120 | bytes 63836904 | solution.py:48
  26.3 7.0 %gather_fusion = bf16[8,2,448,448]{3,2,1,0:T(8,128)(2,1)} fusion(bf16[8,2,448,448]{3,2,1,0:T(8,128)(2,1)} %get-tuple-element.133, s32[1024]{0:T(1024)S(1)} %pad_clamp_fusion.4), kind=kCustom, calls=%fused_computation.clone.1 | custom fusion | bytes 12845088 | tf_op jit(solution)/shard_map/while/body/eval_jaxpr/gather | solution.py:37
  43.1 7.0 %gather_fusion = bf16[8,2,448,448]{3,2,1,0:T(8,128)(2,1)} fusion(bf16[8,2,448,448]{3,2,1,0:T(8,128)(2,1)} %get-tuple-element.133, s32[1024]{0:T(1024)S(1)} %pad_clamp_fusion.4), kind=kCustom, calls=%fused_computation.clone.1 | custom fusion | bytes 12845088 | tf_op jit(solution)/shard_map/while/body/eval_jaxpr/gather | solution.py:37
  51.5 3.5 fusion.68
  59.9 7.0 %gather_fusion = bf16[8,2,448,448]{3,2,1,0:T(8,128)(2,1)} fusion(bf16[8,2,448,448]{3,2,1,0:T(8,128)(2,1)} %get-tuple-element.133, s32[1024]{0:T(1024)S(1)} %pad_clamp_fusion.4), kind=kCustom, calls=%fused_computation.clone.1 | custom fusion | bytes 12845088 | tf_op jit(solution)/shard_map/while/body/eval_jaxpr/gather | solution.py:37
  76.7 7.0 %gather_fusion = bf16[8,2,448,448]{3,2,1,0:T(8,128)(2,1)} fusion(bf16[8,2,448,448]{3,2,1,0:T(8,128)(2,1)} %get-tuple-element.133, s32[1024]{0:T(1024)S(1)} %pad_clamp_fusion.4), kind=kCustom, calls=%fused_computation.clone.1 | custom fusion | bytes 12845088 | tf_op jit(solution)/shard_map/while/body/eval_jaxpr/gather | solution.py:37
  93.5 7.0 %gather_fusion = bf16[8,2,448,448]{3,2,1,0:T(8,128)(2,1)} fusion(bf16[8,2,448,448]{3,2,1,0:T(8,128)(2,1)} %get-tuple-element.133, s32[1024]{0:T(1024)S(1)} %pad_clamp_fusion.4), kind=kCustom, calls=%fused_computation.clone.1 | custom fusion | bytes 12845088 | tf_op jit(solution)/shard_map/while/body/eval_jaxpr/gather | solution.py:37
  110.3 7.0 %gather_fusion = bf16[8,2,448,448]{3,2,1,0:T(8,128)(2,1)} fusion(bf16[8,2,448,448]{3,2,1,0:T(8,128)(2,1)} %get-tuple-element.133, s32[1024]{0:T(1024)S(1)} %pad_clamp_fusion.4), kind=kCustom, calls=%fused_computation.clone.1 | custom fusion | bytes 12845088 | tf_op jit(solution)/shard_map/while/body/eval_jaxpr/gather | solution.py:37
  127.1 7.0 %gather_fusion = bf16[8,2,448,448]{3,2,1,0:T(8,128)(2,1)} fusion(bf16[8,2,448,448]{3,2,1,0:T(8,128)(2,1)} %get-tuple-element.133, s32[1024]{0:T(1024)S(1)} %pad_clamp_fusion.4), kind=kCustom, calls=%fused_computation.clone.1 | custom fusion | bytes 12845088 | tf_op jit(solution)/shard_map/while/body/eval_jaxpr/gather | solution.py:37
  143.9 7.0 %gather_fusion = bf16[8,2,448,448]{3,2,1,0:T(8,128)(2,1)} fusion(bf16[8,2,448,448]{3,2,1,0:T(8,128)(2,1)} %get-tuple-element.133, s32[1024]{0:T(1024)S(1)} %pad_clamp_fusion.4), kind=kCustom, calls=%fused_computation.clone.1 | custom fusion | bytes 12845088 | tf_op jit(solution)/shard_map/while/body/eval_jaxpr/gather | solution.py:37
  160.7 12.3 %gather_fusion.3 = bf16[128,896,64]{1,2,0:T(8,128)(2,1)} fusion(bf16[64,896,64]{1,2,0:T(8,128)(2,1)} %bitcast.33, s32[1024]{0:T(1024)S(1)} %pad_clamp_fusion.2), kind=kCustom, calls=%fused_computation.3 | custom fusion | bytes 29360640 | tf_op jit(solution)/shard_map/gather | solution.py:94
  173.0 13.4 %broadcast_multiply_fusion = bf16[16,8,896,64]{2,3,1,0:T(8,128)(2,1)} fusion(bf16[16,8,896,64]{2,3,1,0:T(8,128)(2,1)} %bitcast.236, bf16[16,8]{1,0:T(8,128)(2,1)S(1)} %convert_element_type.32), kind=kLoop, calls=%fused_computation.29 | loop fusion | flops 7340032 | bytes 29360384 | tf_op jit(solution)/shard_map/mul | solution.py:94
  186.4 6.0 all-to-all-start.1
  194.5 258.1 %all-to-all-done.1 = bf16[16,8,896,64]{2,3,1,0:T(8,128)(2,1)} async-done(((bf16[16,8,896,64]{2,3,1,0:T(8,128)(2,1)}), bf16[16,8,896,64]{2,3,1,0:T(8,128)(2,1)}, u32[]{:S(2)}, u32[]{:S(2)}) %all-to-all-start.1) | async-done | bytes 14680096 | tf_op jit(solution)/shard_map/all_to_all | solution.py:96
  452.6 26.5 %copy.80 = bf16[16,8,896,64]{3,2,1,0:T(8,128)(2,1)} copy(bf16[16,8,896,64]{2,3,1,0:T(8,128)(2,1)} %all-to-all-done.1) | data formatting | bytes 29360128 | tf_op jit(solution)/shard_map/all_to_all | solution.py:96
  479.1 28.1 %reshape_reshape.3 = bf16[128,57344]{1,0:T(8,128)(2,1)} reshape(bf16[16,8,896,64]{3,2,1,0:T(8,128)(2,1)} %copy.80) | data formatting | bytes 29360128 | tf_op jit(solution)/shard_map/reshape;reshape | solution.py:106
  507.2 20.1 %copy.81 = bf16[57344,128]{1,0:T(8,128)(2,1)} copy(bf16[57344,128]{0,1:T(8,128)(2,1)} %bitcast.238) | data formatting | bytes 29360128 | tf_op jit(solution)/shard_map/dot_general | solution.py:104
  527.4 35.5 %fusion.34 = f32[896,16,64]{0,1,2:T(8,128)} fusion(bf16[896,64,128]{2,1,0:T(8,128)(2,1)} %bitcast.237, s32[128]{0:T(128)S(1)} %eq.64), kind=kOutput, calls=%fused_computation.61 | convolution fusion | flops 234883072 | bytes 18350592 | tf_op jit(solution)/shard_map/dot_general | solution.py:104
  562.9 11.4 %add_reduce_fusion = (f32[16,64]{0,1:T(8,128)S(1)}, f32[448,16,64]{0,1,2:T(8,128)}, f32[448,16,64]{0,1,2:T(8,128)}) fusion(f32[448,16,64]{0,2,1:T(8,128)S(1)} %bitcast.241, f32[448,16,64]{0,2,1:T(8,128)} %bitcast.247, f32[448,16,64]{0,2,1:T(8,128)S(1)} %bitcast.243, f32[448,16,64]{0,2,1:T(8,128)S(1)} %bitcast.245, f32[16,64]{0,1:T(8,128)S(1)} %copy.87, ...), kind=kLoop, calls=%fused_computation.60 | loop fusion | flops 8256512 | bytes 14692352 | tf_op jit(solution)/shard_map/reduce_sum | solution.py:123
  578.4 20.3 %collective-permute-start.1 = (f32[32]{0:T(128)S(1)}, f32[32]{0:T(128)S(1)}, u32[]{:S(2)}, u32[]{:S(2)}) collective-permute-start(f32[32]{0:T(128)S(1)} %add.156), channel_id=1, source_target_pairs={{0,2},{1,3},{2,0},{3,1},{4,6},{5,7},{6,4},{7,5},{8,10},{9,11},{10,... | collective-permute-start | bytes 392 | tf_op jit(solution)/shard_map/ppermute | solution.py:126
  600.3 39.3 %collective-permute-start.2 = (f32[32]{0:T(128)S(1)}, f32[32]{0:T(128)S(1)}, u32[]{:S(2)}, u32[]{:S(2)}) collective-permute-start(f32[32]{0:T(128)S(1)} %add.157), channel_id=1, source_target_pairs={{0,4},{1,5},{2,6},{3,7},{4,0},{5,1},{6,2},{7,3},{8,12},{9,13},{10,... | collective-permute-start | bytes 392 | tf_op jit(solution)/shard_map/ppermute | solution.py:126
  641.2 3.5 collective-permute-start.3
  (205 shorter events, 101.2 us)
Async XLA Ops:
  0.6 15.6 %copy-start = (f32[2,448,256]{2,1,0:T(8,128)S(1)}, f32[2,448,256]{2,1,0:T(8,128)}, u32[]{:S(2)}) copy-start(f32[2,448,256]{2,1,0:T(8,128)} %param.14) | copy-start | bytes 2752516
  0.6 16.9 %copy-start.21 = (s32[64]{0:T(128)S(1)}, s32[64]{0:T(128)}, u32[]{:S(2)}) copy-start(s32[64]{0:T(128)} %param.19) | copy-start | bytes 772
  0.7 16.9 %copy-start.20 = (s32[64]{0:T(128)S(1)}, s32[64]{0:T(128)}, u32[]{:S(2)}) copy-start(s32[64]{0:T(128)} %param.21) | copy-start | bytes 772
  0.7 17.0 %copy-start.19 = (f32[2,448,32]{1,2,0:T(8,128)S(1)}, f32[2,448,32]{1,2,0:T(8,128)}, u32[]{:S(2)}) copy-start(f32[2,448,32]{1,2,0:T(8,128)} %param.16) | copy-start | bytes 344068
  5.5 180.9 %all-to-all-start = ((s32[16,1,8]{2,1,0:T(1,128)}), s32[16,1,8]{2,1,0:T(1,128)S(1)}, u32[]{:S(2)}, u32[]{:S(2)}) async-start(s32[16,1,8]{2,1,0:T(1,128)} %bitcast.24), calls=%async_computation | async-start | bytes 16384 | tf_op jit(solution)/shard_map/all_to_all | solution.py:97
  33.3 4.9 copy-start.2
  50.1 4.9 copy-start.2
  67.0 4.9 copy-start.2
  100.5 4.9 copy-start.2
  117.3 4.9 copy-start.2
  134.1 4.9 copy-start.2
  186.4 266.2 %all-to-all-start.1 = ((bf16[16,8,896,64]{2,3,1,0:T(8,128)(2,1)}), bf16[16,8,896,64]{2,3,1,0:T(8,128)(2,1)}, u32[]{:S(2)}, u32[]{:S(2)}) async-start(bf16[16,8,896,64]{2,3,1,0:T(8,128)(2,1)} %broadcast_multiply_fusion), calls=%async_computation.1 | async-start | bytes 29360128 | tf_op jit(solution)/shard_map/all_to_all | solution.py:96
  527.4 35.5 %copy-start.4 = (f32[448,32,32]{0,2,1:T(8,128)S(1)}, f32[448,32,32]{0,2,1:T(8,128)}, u32[]{:S(2)}) copy-start(f32[448,32,32]{0,2,1:T(8,128)} %copy-done.3) | copy-start | bytes 5505028
  527.4 35.5 %copy-start.6 = (f32[448,32,32]{0,2,1:T(8,128)S(1)}, f32[448,32,32]{0,2,1:T(8,128)}, u32[]{:S(2)}) copy-start(f32[448,32,32]{0,2,1:T(8,128)} %copy-done.5) | copy-start | bytes 5505028
  527.4 35.5 %copy-start.8 = (f32[448,32,32]{0,2,1:T(8,128)S(1)}, f32[448,32,32]{0,2,1:T(8,128)}, u32[]{:S(2)}) copy-start(f32[448,32,32]{0,2,1:T(8,128)} %copy-done.7) | copy-start | bytes 5505028
  574.4 4.0 collective-permute-start
  575.4 23.3 %copy-start.10 = (f32[448,16,64]{0,1,2:T(8,128)S(1)}, f32[448,16,64]{0,1,2:T(8,128)}, u32[]{:S(2)}) copy-start(f32[448,16,64]{0,1,2:T(8,128)} %get-tuple-element.69) | copy-start | bytes 5505028
  578.4 21.8 %collective-permute-start.1 = (f32[32]{0:T(128)S(1)}, f32[32]{0:T(128)S(1)}, u32[]{:S(2)}, u32[]{:S(2)}) collective-permute-start(f32[32]{0:T(128)S(1)} %add.156), channel_id=1, source_target_pairs={{0,2},{1,3},{2,0},{3,1},{4,6},{5,7},{6,4},{7,5},{8,10},{9,11},{10,... | collective-permute-start | bytes 392 | tf_op jit(solution)/shard_map/ppermute | solution.py:126
  598.7 40.9 %copy-start.12 = (f32[448,32]{0,1:T(8,128)S(1)}, f32[448,32]{0,1:T(8,128)}, u32[]{:S(2)}) copy-start(f32[448,32]{0,1:T(8,128)} %copy-done.11) | copy-start | bytes 172036
  598.7 40.9 %copy-start.14 = (f32[448,32]{0,1:T(8,128)S(1)}, f32[448,32]{0,1:T(8,128)}, u32[]{:S(2)}) copy-start(f32[448,32]{0,1:T(8,128)} %copy-done.13) | copy-start | bytes 172036
  598.7 40.9 %copy-start.16 = (f32[448,32]{0,1:T(8,128)S(1)}, f32[448,32]{0,1:T(8,128)}, u32[]{:S(2)}) copy-start(f32[448,32]{0,1:T(8,128)} %copy-done.15) | copy-start | bytes 172036
  598.7 40.9 %copy-start.18 = (f32[448,32]{0,1:T(8,128)S(1)}, f32[448,32]{0,1:T(8,128)}, u32[]{:S(2)}) copy-start(f32[448,32]{0,1:T(8,128)} %copy-done.17) | copy-start | bytes 172036
  600.3 41.0 %collective-permute-start.2 = (f32[32]{0:T(128)S(1)}, f32[32]{0:T(128)S(1)}, u32[]{:S(2)}, u32[]{:S(2)}) collective-permute-start(f32[32]{0:T(128)S(1)} %add.157), channel_id=1, source_target_pairs={{0,4},{1,5},{2,6},{3,7},{4,0},{5,1},{6,2},{7,3},{8,12},{9,13},{10,... | collective-permute-start | bytes 392 | tf_op jit(solution)/shard_map/ppermute | solution.py:126
  641.2 6.5 collective-permute-start.3
  (11 other events, 24.0 us)
